TPU v7x, 512 devices: a whole 4x8x8 slice. The times are simulated.
512 devices in a mesh: col: 64 (over y_hi, x, z), tok: 8 (over y_lo, core).
Axes of the slice: x: 4, y: 8 (y_hi: 2, y_lo: 4; y = y_hi * 4 + y_lo), z: 8, core: 2. Of those that a mesh axis runs over, the one named last changes fastest.
Arguments:
- acts: bfloat16 [2048, 8192], P('tok', 'col'), may hold values from -6 to 6
- grad_out: bfloat16 [2048, 8192], P('tok', 'col'), may hold values from -0.19921875 to 0.19921875
- left_factor: float32 [8, 8192, 1024], P('tok', 'col'), may hold values from -6 to 6
- right_factor: float32 [8, 8192, 1024], P('tok', 'col'), may hold values from -6 to 6
- left_basis: bfloat16 [8, 8192, 1024], P('tok', 'col'), may hold values from -0.1875 to 0.1875
- right_basis: bfloat16 [8, 8192, 1024], P('tok', 'col'), may hold values from -0.1875 to 0.1875
- moment: float32 [8192, 8192], P('tok', 'col'), may hold values from -2 to 2
- second: float32 [8192, 8192], P('tok', 'col'), may hold values from 0.05 to 2
Outputs:
- left_out: float32 [8, 8192, 1024], P('tok', 'col')
- right_out: float32 [8, 8192, 1024], P('tok', 'col')
- moment_out: float32 [8192, 8192], P('tok', 'col')
- second_out: float32 [8192, 8192], P('tok', 'col')
- update: bfloat16 [8192, 8192], P('tok', 'col')
All inputs are finite; a program needn't handle non-finite values.
Results may differ from a plain program's by a relative error of at most 0.0075.
Values may be sent and summed in bfloat16 or wider, within the bound.
A program may use at most 64 MiB of HBM per device.

v0:
```python
import jax
import jax.numpy as jnp
from jax import lax
from jax.sharding import PartitionSpec as P

B = 1024


shampoo_beta = 0.95
first_beta = 0.9
second_beta = 0.95
first_corr = 1.0 - 0.9**4
second_corr = 1.0 - 0.95**4
epsilon = 1e-08


def swapped(array, axis, distance):
    return lax.ppermute(array, axis, [(i, i ^ 1 << distance) for i in range(lax.axis_size(axis))])


def join_pair(current, incoming, axis, lower):
    width = current.shape[axis]
    shape = list(current.shape)
    shape[axis] = 2 * width
    joined = jnp.zeros(shape, current.dtype)
    mine_at = jnp.where(lower, 0, width)
    theirs_at = width - mine_at
    joined = lax.dynamic_update_slice_in_dim(joined, current, mine_at, axis)
    return lax.dynamic_update_slice_in_dim(joined, incoming, theirs_at, axis)


def shards(acts, grad_out, left_factor, right_factor, left_basis, right_basis, moment, second):
    width = grad_out.shape[1]
    blocks = left_factor.shape[0]
    groups = B // width
    nbits = groups.bit_length() - 1
    member = lax.axis_index("col") % groups
    contract = (((0,), (0,)), ((), ()))
    term = lax.dot_general(
        lax.all_gather(acts, "col", axis=1, tiled=True),
        grad_out,
        contract,
        preferred_element_type=jnp.float32,
    )
    grad = lax.psum_scatter(term, "tok", scatter_dimension=0, tiled=True)
    own = grad.astype(jnp.bfloat16).reshape(blocks, B, width)
    tiles, left_full, right_full = (own, left_basis, right_basis)
    for bit in range(nbits):
        other = swapped((tiles, left_full, right_full), "col", bit)
        lower = member >> bit & 1 == 0
        tiles = join_pair(tiles, other[0], 2, lower)
        left_full = join_pair(left_full, other[1], 1, lower)
        right_full = join_pair(right_full, other[2], 1, lower)
    right_cols = lax.dynamic_slice_in_dim(right_full, member * width, width, 2)
    mixed = jnp.einsum(
        "nab,nbc->nac", tiles, right_cols, preferred_element_type=jnp.float32
    ).astype(jnp.bfloat16)
    lead = lax.dynamic_slice_in_dim(tiles, member * width, width, 1)
    left_new = shampoo_beta * left_factor + (1.0 - shampoo_beta) * jnp.einsum(
        "nab,ncb->nac", lead, tiles, preferred_element_type=jnp.float32
    )
    right_new = shampoo_beta * right_factor + (1.0 - shampoo_beta) * jnp.einsum(
        "nat,nab->ntb", own, tiles, preferred_element_type=jnp.float32
    )
    rotated = jnp.einsum("nab,nac->nbc", left_full, mixed, preferred_element_type=jnp.float32)
    first_new = first_beta * moment.reshape(blocks, B, width) + (1.0 - first_beta) * rotated
    second_new = (
        second_beta * second.reshape(blocks, B, width) + (1.0 - second_beta) * rotated * rotated
    )
    normed = (first_new / first_corr / (jnp.sqrt(second_new / second_corr) + epsilon)).astype(
        jnp.bfloat16
    )
    steps_full = normed
    for bit in range(nbits):
        other_steps = swapped(steps_full, "col", bit)
        lower = member >> bit & 1 == 0
        steps_full = join_pair(steps_full, other_steps, 2, lower)
    back = jnp.einsum(
        "nab,ncb->nac", steps_full, right_basis, preferred_element_type=jnp.float32
    ).astype(jnp.bfloat16)
    update = jnp.einsum("nab,nbc->nac", left_full, back, preferred_element_type=jnp.float32).astype(
        jnp.bfloat16
    )
    rows = blocks * B
    return (
        left_new,
        right_new,
        first_new.reshape(rows, width),
        second_new.reshape(rows, width),
        update.reshape(rows, width),
    )


def solution(mesh):
    in_specs = (
        P("tok", "col"),
        P("tok", "col"),
        P("tok", "col", None),
        P("tok", "col", None),
        P("tok", "col", None),
        P("tok", "col", None),
        P("tok", "col"),
        P("tok", "col"),
    )
    out_specs = (
        P("tok", "col", None),
        P("tok", "col", None),
        P("tok", "col"),
        P("tok", "col"),
        P("tok", "col"),
    )
    return jax.shard_map(shards, mesh=mesh, in_specs=in_specs, out_specs=out_specs, check_vma=False)
```

profile of v0, /device:TPU:9, one launch (start us, length us, event | category | flops | bytes accessed | tf_op | source)
XLA Modules:
  0.0 488.8 jit_solution(3307319483804612024)
XLA Ops:
  8.0 126.3 %all-gather.2.cloned.1.call-done = bf16[256,8192]{1,0:T(8,128)(2,1)} async-done(((bf16[256,128]{1,0:T(8,128)(2,1)}), bf16[256,8192]{1,0:T(8,128)(2,1)}) %all-gather.2.cloned.1.call-update) | async-done | bytes 4194320 | tf_op jit(solution)/shard_map/all_gather | solution.py:40
  134.3 5.4 %fusion.50 = f32[8192,128]{1,0:T(8,128)} fusion(bf16[256,8192]{1,0:T(8,128)(2,1)} %all-gather.2.cloned.1.call-done, bf16[256,128]{1,0:T(8,128)(2,1)S(1)} %copy-done), kind=kOutput, calls=%fused_computation.54 | convolution fusion | flops 536870912 | bytes 8454144 | tf_op jit(solution)/shard_map/dot_general | solution.py:39
  140.7 1.9 collective-permute-start.6
  142.6 3.4 collective-permute-start.3
  146.1 1.7 collective-permute-done.6
  147.8 2.3 collective-permute-start.7
  150.2 2.5 collective-permute-done.3
  152.7 1.9 collective-permute-start.4
  154.6 44.9 %reduce-scatter.2.cloned.1.call-done = f32[1024,128]{1,0:T(8,128)} async-done(((f32[8192,128]{1,0:T(8,128)}), f32[1024,128]{1,0:T(8,128)}) %reduce-scatter.2.cloned.1.call-update) | async-done | bytes 524304 | tf_op jit(solution)/shard_map/reduce_scatter | solution.py:45
  200.4 1.9 constant_dynamic-update-slice_fusion.19
  202.3 3.2 collective-permute-start
  205.8 6.8 %collective-permute-start.8 = (bf16[1,512,1024]{2,1,0:T(8,128)(2,1)S(1)}, bf16[1,512,1024]{2,1,0:T(8,128)(2,1)}, u32[]{:S(2)}, u32[]{:S(2)}) collective-permute-start(bf16[1,512,1024]{2,1,0:T(8,128)(2,1)S(1)} %constant_dynamic-update-slice_fusion.6), channel_id=1, source_target_pairs={{0,32},{8,40},{16,48},{24,56},{32,0},{40,8},{48,16},{56,24},{64,96... | collective-permute-start | bytes 3145736 | tf_op jit(solution)/shard_map/ppermute | solution.py:18
  212.7 1.7 constant_dynamic-update-slice_fusion.18
  214.3 3.4 collective-permute-start.1
  218.0 7.8 %collective-permute-start.5 = (bf16[1,512,1024]{2,1,0:T(8,128)(2,1)S(1)}, bf16[1,512,1024]{2,1,0:T(8,128)(2,1)}, u32[]{:S(2)}, u32[]{:S(2)}) collective-permute-start(bf16[1,512,1024]{2,1,0:T(8,128)(2,1)S(1)} %constant_dynamic-update-slice_fusion.10), channel_id=1, source_target_pairs={{0,32},{8,40},{16,48},{24,56},{32,0},{40,8},{48,16},{56,24},{64,96... | collective-permute-start | bytes 3145736 | tf_op jit(solution)/shard_map/ppermute | solution.py:18
  225.9 1.1 constant_dynamic-update-slice_fusion.17
  227.0 100.2 %collective-permute-done.1 = bf16[1,1024,256]{2,1,0:T(8,128)(2,1)S(1)} collective-permute-done((bf16[1,1024,256]{2,1,0:T(8,128)(2,1)}, bf16[1,1024,256]{2,1,0:T(8,128)(2,1)S(1)}, u32[]{:S(2)}, u32[]{:S(2)}) %collective-permute-start.1) | collective-permute-done | bytes 524320 | tf_op jit(solution)/shard_map/ppermute | solution.py:18
  327.2 5.2 %collective-permute-start.2 = (bf16[1,1024,512]{2,1,0:T(8,128)(2,1)S(1)}, bf16[1,1024,512]{2,1,0:T(8,128)(2,1)}, u32[]{:S(2)}, u32[]{:S(2)}) collective-permute-start(bf16[1,1024,512]{2,1,0:T(8,128)(2,1)S(1)} %constant_dynamic-update-slice_fusion.16), channel_id=1, source_target_pairs={{0,32},{8,40},{16,48},{24,56},{32,0},{40,8},{48,16},{56,24},{64,96... | collective-permute-start | bytes 3145736 | tf_op jit(solution)/shard_map/ppermute | solution.py:18
  333.2 1.3 constant_dynamic-update-slice_fusion.4
  334.5 2.1 bitcast_dynamic-update-slice_fusion.2
  337.9 42.3 %collective-permute-done.2 = bf16[1,1024,512]{2,1,0:T(8,128)(2,1)} collective-permute-done((bf16[1,1024,512]{2,1,0:T(8,128)(2,1)S(1)}, bf16[1,1024,512]{2,1,0:T(8,128)(2,1)}, u32[]{:S(2)}, u32[]{:S(2)}) %collective-permute-start.2) | collective-permute-done | bytes 1048608 | tf_op jit(solution)/shard_map/ppermute | solution.py:18
  380.3 1.4 constant_dynamic-update-slice_fusion.14
  381.7 5.3 %constant_dynamic-update-slice_fusion.3 = (bf16[1,1024,256]{2,1,0:T(8,128)(2,1)S(1)}, bf16[1,1024,128]{2,1,0:T(8,128)(2,1)S(1)}, f32[1024,128]{1,0:T(8,128)}, f32[1024,128]{1,0:T(8,128)}) fusion(bf16[1,1024,256]{2,1,0:T(8,128)(2,1)S(1)} %broadcast.41, s32[]{:T(128)S(6)} %select_n.61, f32[1024,128]{1,0:T(8,128)} %param.15, f32[1024,128]{1,0:T(8,128)} %param.14, ...), kind=kOutput, calls=%fused_computation.35 | convolution fusion | flops 538574848 | bytes 7077896 | tf_op jit(solution)/shard_map/nab,nac->nbc/dot_general | solution.py:65
  387.1 2.0 collective-permute-start.9
  389.1 7.0 %collective-permute-done.9 = bf16[1,1024,128]{2,1,0:T(8,128)(2,1)S(1)} collective-permute-done((bf16[1,1024,128]{2,1,0:T(8,128)(2,1)S(1)}, bf16[1,1024,128]{2,1,0:T(8,128)(2,1)S(1)}, u32[]{:S(2)}, u32[]{:S(2)}) %collective-permute-start.9) | collective-permute-done | bytes 262176 | tf_op jit(solution)/shard_map/ppermute | solution.py:18
  396.1 2.8 collective-permute-start.10
  399.1 24.9 %collective-permute-done.10 = bf16[1,1024,256]{2,1,0:T(8,128)(2,1)S(1)} collective-permute-done((bf16[1,1024,256]{2,1,0:T(8,128)(2,1)S(1)}, bf16[1,1024,256]{2,1,0:T(8,128)(2,1)S(1)}, u32[]{:S(2)}, u32[]{:S(2)}) %collective-permute-start.10) | collective-permute-done | bytes 524320 | tf_op jit(solution)/shard_map/ppermute | solution.py:18
  424.0 5.1 %collective-permute-start.11 = (bf16[1,1024,512]{2,1,0:T(8,128)(2,1)S(1)}, bf16[1,1024,512]{2,1,0:T(8,128)(2,1)S(1)}, u32[]{:S(2)}, u32[]{:S(2)}) collective-permute-start(bf16[1,1024,512]{2,1,0:T(8,128)(2,1)S(1)} %constant_dynamic-update-slice_fusion), channel_id=1, source_target_pairs={{0,32},{8,40},{16,48},{24,56},{32,0},{40,8},{48,16},{56,24},{64,96... | collective-permute-start | bytes 3145736 | tf_op jit(solution)/shard_map/ppermute | solution.py:18
  429.2 1.6 fusion.21
  430.8 1.3 fusion.18
  432.5 44.8 %collective-permute-done.11 = bf16[1,1024,512]{2,1,0:T(8,128)(2,1)S(1)} collective-permute-done((bf16[1,1024,512]{2,1,0:T(8,128)(2,1)S(1)}, bf16[1,1024,512]{2,1,0:T(8,128)(2,1)S(1)}, u32[]{:S(2)}, u32[]{:S(2)}) %collective-permute-start.11) | collective-permute-done | bytes 1048608 | tf_op jit(solution)/shard_map/ppermute | solution.py:18
  477.5 4.5 convolution_convert_fusion
  (54 shorter events, 6.1 us)
Async XLA Ops:
  7.2 127.1 %copy-start = (bf16[256,128]{1,0:T(8,128)(2,1)S(1)}, bf16[256,128]{1,0:T(8,128)(2,1)}, u32[]{:S(2)}) copy-start(bf16[256,128]{1,0:T(8,128)(2,1)} %param.9) | copy-start | bytes 196612
  7.2 127.1 %all-gather.2.cloned.1.call-start = ((), (), s32[]{:S(2)}) async-start(), calls=%async_computation.1 | async-start | bytes 4259840 | tf_op jit(solution)/shard_map/all_gather | solution.py:40
  7.9 191.7 %reduce-scatter.2.cloned.1.call-start = ((), (), s32[]{:S(2)}) async-start(), calls=%async_computation.2 | async-start | bytes 4718592 | tf_op jit(solution)/shard_map/reduce_scatter | solution.py:45
  139.7 0.9 copy-start.7
  139.7 2.9 copy-start.6
  140.7 7.1 %collective-permute-start.6 = (bf16[1,128,1024]{2,1,0:T(8,128)(2,1)S(1)}, bf16[1,128,1024]{2,1,0:T(8,128)(2,1)S(1)}, u32[]{:S(2)}, u32[]{:S(2)}) collective-permute-start(bf16[1,128,1024]{2,1,0:T(8,128)(2,1)S(1)} %copy-done.7), channel_id=1, source_target_pairs={{0,8},{8,0},{16,24},{24,16},{32,40},{40,32},{48,56},{56,48},{64,72... | collective-permute-start | bytes 786440 | tf_op jit(solution)/shard_map/ppermute | solution.py:18
  142.6 10.1 %collective-permute-start.3 = (bf16[1,128,1024]{2,1,0:T(8,128)(2,1)S(1)}, bf16[1,128,1024]{2,1,0:T(8,128)(2,1)S(1)}, u32[]{:S(2)}, u32[]{:S(2)}) collective-permute-start(bf16[1,128,1024]{2,1,0:T(8,128)(2,1)S(1)} %copy-done.6), channel_id=1, source_target_pairs={{0,8},{8,0},{16,24},{24,16},{32,40},{40,32},{48,56},{56,48},{64,72... | collective-permute-start | bytes 786440 | tf_op jit(solution)/shard_map/ppermute | solution.py:18
  147.8 58.0 %collective-permute-start.7 = (bf16[1,256,1024]{2,1,0:T(8,128)(2,1)S(1)}, bf16[1,256,1024]{2,1,0:T(8,128)(2,1)S(1)}, u32[]{:S(2)}, u32[]{:S(2)}) collective-permute-start(bf16[1,256,1024]{2,1,0:T(8,128)(2,1)S(1)} %constant_dynamic-update-slice_fusion.8), channel_id=1, source_target_pairs={{0,16},{8,24},{16,0},{24,8},{32,48},{40,56},{48,32},{56,40},{64,80... | collective-permute-start | bytes 1572872 | tf_op jit(solution)/shard_map/ppermute | solution.py:18
  152.7 65.3 %collective-permute-start.4 = (bf16[1,256,1024]{2,1,0:T(8,128)(2,1)S(1)}, bf16[1,256,1024]{2,1,0:T(8,128)(2,1)S(1)}, u32[]{:S(2)}, u32[]{:S(2)}) collective-permute-start(bf16[1,256,1024]{2,1,0:T(8,128)(2,1)S(1)} %constant_dynamic-update-slice_fusion.12), channel_id=1, source_target_pairs={{0,16},{8,24},{16,0},{24,8},{32,48},{40,56},{48,32},{56,40},{64,80... | collective-permute-start | bytes 1572872 | tf_op jit(solution)/shard_map/ppermute | solution.py:18
  202.3 10.4 %collective-permute-start = (bf16[1,1024,128]{2,1,0:T(8,128)(2,1)}, bf16[1,1024,128]{2,1,0:T(8,128)(2,1)}, u32[]{:S(2)}, u32[]{:S(2)}) collective-permute-start(bf16[1,1024,128]{2,1,0:T(8,128)(2,1)} %get-tuple-element.10), channel_id=1, source_target_pairs={{0,8},{8,0},{16,24},{24,16},{32,40},{40,32},{48,56},{56,48},{64,72... | collective-permute-start | bytes 786440 | tf_op jit(solution)/shard_map/ppermute | solution.py:18
  205.8 127.3 %collective-permute-start.8 = (bf16[1,512,1024]{2,1,0:T(8,128)(2,1)S(1)}, bf16[1,512,1024]{2,1,0:T(8,128)(2,1)}, u32[]{:S(2)}, u32[]{:S(2)}) collective-permute-start(bf16[1,512,1024]{2,1,0:T(8,128)(2,1)S(1)} %constant_dynamic-update-slice_fusion.6), channel_id=1, source_target_pairs={{0,32},{8,40},{16,48},{24,56},{32,0},{40,8},{48,16},{56,24},{64,96... | collective-permute-start | bytes 3145736 | tf_op jit(solution)/shard_map/ppermute | solution.py:18
  214.3 112.8 %collective-permute-start.1 = (bf16[1,1024,256]{2,1,0:T(8,128)(2,1)}, bf16[1,1024,256]{2,1,0:T(8,128)(2,1)S(1)}, u32[]{:S(2)}, u32[]{:S(2)}) collective-permute-start(bf16[1,1024,256]{2,1,0:T(8,128)(2,1)} %constant_dynamic-update-slice_fusion.18), channel_id=1, source_target_pairs={{0,16},{8,24},{16,0},{24,8},{32,48},{40,56},{48,32},{56,40},{64,80... | collective-permute-start | bytes 1572872 | tf_op jit(solution)/shard_map/ppermute | solution.py:18
  218.0 116.5 %collective-permute-start.5 = (bf16[1,512,1024]{2,1,0:T(8,128)(2,1)S(1)}, bf16[1,512,1024]{2,1,0:T(8,128)(2,1)}, u32[]{:S(2)}, u32[]{:S(2)}) collective-permute-start(bf16[1,512,1024]{2,1,0:T(8,128)(2,1)S(1)} %constant_dynamic-update-slice_fusion.10), channel_id=1, source_target_pairs={{0,32},{8,40},{16,48},{24,56},{32,0},{40,8},{48,16},{56,24},{64,96... | collective-permute-start | bytes 3145736 | tf_op jit(solution)/shard_map/ppermute | solution.py:18
  327.2 53.1 %collective-permute-start.2 = (bf16[1,1024,512]{2,1,0:T(8,128)(2,1)S(1)}, bf16[1,1024,512]{2,1,0:T(8,128)(2,1)}, u32[]{:S(2)}, u32[]{:S(2)}) collective-permute-start(bf16[1,1024,512]{2,1,0:T(8,128)(2,1)S(1)} %constant_dynamic-update-slice_fusion.16), channel_id=1, source_target_pairs={{0,32},{8,40},{16,48},{24,56},{32,0},{40,8},{48,16},{56,24},{64,96... | collective-permute-start | bytes 3145736 | tf_op jit(solution)/shard_map/ppermute | solution.py:18
  334.5 2.4 copy-start.1
  336.6 1.3 copy-start.2
  387.1 42.1 %copy-start.5 = (f32[1,128,1024]{2,1,0:T(8,128)S(1)}, f32[1,128,1024]{2,1,0:T(8,128)}, u32[]{:S(2)}) copy-start(f32[1,128,1024]{2,1,0:T(8,128)} %param.10) | copy-start | bytes 1572868
  387.1 9.0 %collective-permute-start.9 = (bf16[1,1024,128]{2,1,0:T(8,128)(2,1)S(1)}, bf16[1,1024,128]{2,1,0:T(8,128)(2,1)S(1)}, u32[]{:S(2)}, u32[]{:S(2)}) collective-permute-start(bf16[1,1024,128]{2,1,0:T(8,128)(2,1)S(1)} %get-tuple-element.6), channel_id=1, source_target_pairs={{0,8},{8,0},{16,24},{24,16},{32,40},{40,32},{48,56},{56,48},{64,72... | collective-permute-start | bytes 786440 | tf_op jit(solution)/shard_map/ppermute | solution.py:18
  396.1 27.9 %collective-permute-start.10 = (bf16[1,1024,256]{2,1,0:T(8,128)(2,1)S(1)}, bf16[1,1024,256]{2,1,0:T(8,128)(2,1)S(1)}, u32[]{:S(2)}, u32[]{:S(2)}) collective-permute-start(bf16[1,1024,256]{2,1,0:T(8,128)(2,1)S(1)} %constant_dynamic-update-slice_fusion.2), channel_id=1, source_target_pairs={{0,16},{8,24},{16,0},{24,8},{32,48},{40,56},{48,32},{56,40},{64,80... | collective-permute-start | bytes 1572872 | tf_op jit(solution)/shard_map/ppermute | solution.py:18
  399.1 31.7 %copy-start.3 = (f32[1024,128]{1,0:T(8,128)S(1)}, f32[1024,128]{1,0:T(8,128)}, u32[]{:S(2)}) copy-start(f32[1024,128]{1,0:T(8,128)} %reduce-scatter.2.cloned.1.call-done) | copy-start | bytes 1572868
  399.1 31.7 %copy-start.4 = (f32[1,128,1024]{2,1,0:T(8,128)S(1)}, f32[1,128,1024]{2,1,0:T(8,128)}, u32[]{:S(2)}) copy-start(f32[1,128,1024]{2,1,0:T(8,128)} %param.11) | copy-start | bytes 1572868
  424.0 53.3 %collective-permute-start.11 = (bf16[1,1024,512]{2,1,0:T(8,128)(2,1)S(1)}, bf16[1,1024,512]{2,1,0:T(8,128)(2,1)S(1)}, u32[]{:S(2)}, u32[]{:S(2)}) collective-permute-start(bf16[1,1024,512]{2,1,0:T(8,128)(2,1)S(1)} %constant_dynamic-update-slice_fusion), channel_id=1, source_target_pairs={{0,32},{8,40},{16,48},{24,56},{32,0},{40,8},{48,16},{56,24},{64,96... | collective-permute-start | bytes 3145736 | tf_op jit(solution)/shard_map/ppermute | solution.py:18
Sparse Core Ops, SparseCore 0:
  12.3 121.9 all-gather.1
  139.9 59.6 reduce-scatter.1
where the time goes:
time: 490 us; the launch traced here: 489 us
  waiting for transfers between devices  395 us (81%)
  starting transfers between devices  46 us (9%)
  matrix products  18.2 us (4%)
  between operations  14.5 us (3%)
  local copies, waits for them, and re-layouts  12.9 us (3%)
    ppermute x12, waiting for transfers between devices, swapped(): lax.ppermute(array, axis, [(i, i ^ 1 << distance) for i in range(lax.axis...  223 us
    all_gather x1, waiting for transfers between devices, shards(): lax.all_gather(acts, 'col', axis=1, tiled=True)  126 us
    ppermute x12, starting transfers between devices, swapped(): lax.ppermute(array, axis, [(i, i ^ 1 << distance) for i in range(lax.axis...  45.9 us
    reduce_scatter x1, waiting for transfers between devices, shards(): grad = lax.psum_scatter(term, 'tok', scatter_dimension=0, tiled=True)  44.9 us
  transfers between devices with their start and end apart: 14, of which 9 were waited for; matrix products, arithmetic and copies ran while one was open for 3% of the time, Pallas kernels for 0%

commit v1 on v0

v1 whole, which is shorter than its diff:
```python
import jax
import jax.numpy as jnp
from jax import lax
from jax.experimental import pallas as pl
from jax.experimental.pallas import tpu as pltpu
from jax.sharding import PartitionSpec as P

MESH = pl.DeviceIdType.MESH
F32 = jnp.float32
BF16 = jnp.bfloat16

shampoo_beta = 0.95
first_beta = 0.9
second_beta = 0.95
first_corr = 1.0 - 0.9**4
second_corr = 1.0 - 0.95**4
epsilon = 1e-08

B = 1024
W = 128
T = 256
N = 8


def dot_nn(a, b):
    return lax.dot_general(a, b, (((1,), (0,)), ((), ())), preferred_element_type=F32)


def dot_nt(a, b):
    return lax.dot_general(a, b, (((1,), (1,)), ((), ())), preferred_element_type=F32)


def lanes(k, size=W):
    return pl.ds(pl.multiple_of(k * size, size), size)


class Ring:
    def __init__(self, buf, send, recv, z, at, half):
        self.buf, self.send, self.recv, self.z, self.at, self.half = buf, send, recv, z, at, half

    @staticmethod
    def valid(s, h, way):
        return s < 3 or h == way

    def copy(self, s, h, way, slot, to):
        ref = self.buf.at[slot, self.half(h)]
        return pltpu.make_async_remote_copy(
            src_ref=ref,
            dst_ref=ref,
            send_sem=self.send.at[way, s, h],
            recv_sem=self.recv.at[way, s, h],
            device_id=self.at(to),
            device_id_type=MESH,
        )

    def outgoing(self, s, h, way):
        slot = lax.rem(self.z + (N - s if way == 0 else s), N)
        to = lax.rem(self.z + (1 if way == 0 else N - 1), N)
        return self.copy(s, h, way, slot, to)

    def incoming(self, s, h, way):
        slot = lax.rem(self.z + (N - 1 - s if way == 0 else 1 + s), N)
        to = lax.rem(self.z + (1 if way == 0 else N - 1), N)
        return self.copy(s, h, way, slot, to)

    def start(self, h):
        for way in range(2):
            self.outgoing(0, h, way).start()

    def forward(self, s, h):
        for way in range(2):
            if self.valid(s, h, way):
                self.incoming(s, h, way).wait_recv()
                if s < 3 and self.valid(s + 1, h, way):
                    self.outgoing(s + 1, h, way).start()

    def finish(self):
        for s in range(4):
            for h in range(2):
                for way in range(2):
                    if self.valid(s, h, way):
                        self.outgoing(s, h, way).wait_send()


def kernel(
    acts_in, go_in, lf_in, rf_in, ql_in, qr_in, mo_in, se_in,
    lo_out, ro_out, mo_out, se_out, up_out,
    acts_v, acts_b, at_v, go_b, psend, pown, d2d, ysend, yrecv,
    ql_b, qr_v, qrc, qrct, g_b, mixt, mo_v, se_v, lf_v, rf_v, n_b, back_v, up_v,
    load_sem, store_sem,
    ya_send, ya_recv, xa_send, xa_recv, gx_send, gx_recv, qr_send, qr_recv,
    dd_send, dd_recv, yy_send, yy_recv,
    go_rs, go_rr, ql_rs, ql_rr, g_rs, g_rr, n_rs, n_rr,
):
    tok, col = lax.axis_index("tok"), lax.axis_index("col")
    z, blk = lax.rem(col, N), lax.div(col, N)
    y_hi, x = lax.div(blk, 4), lax.rem(blk, 4)
    p, q = lax.div(tok, 4), lax.rem(tok, 4)
    a, core = lax.div(q, 2), lax.rem(q, 2)

    def dev(col_, tok_):
        return {"col": col_, "tok": tok_}

    def in_ring(z_):
        return dev(blk * N + z_, tok)

    def in_quad(p_, y_hi_):
        return dev((y_hi_ * 4 + x) * N + z, p_ * 4 + q)

    def in_row(x_):
        return dev((y_hi * 4 + x_) * N + z, tok)

    other_core = dev(col, p * 4 + a * 2 + 1 - core)
    other_y = dev(col, p * 4 + (1 - a) * 2 + core)

    def load(src, dst, n):
        c = pltpu.make_async_copy(src, dst, load_sem.at[n])
        c.start()
        return c

    go_load = load(go_in, go_b.at[z, p], 0)
    acts_load = load(acts_in, acts_v, 1)
    ql_load = [load(ql_in.at[0, pl.ds(64 * h, 64)], ql_b.at[z, h], 2 + h) for h in range(2)]
    qr_load = load(qr_in.at[0], qr_v, 4)
    late_loads = [
        load(mo_in, mo_v, 5),
        load(se_in, se_v, 6),
        load(lf_in.at[0], lf_v, 7),
        load(rf_in.at[0], rf_v, 8),
    ]

    barrier = pltpu.get_barrier_semaphore()
    partners = [in_ring(lax.rem(z + d, N)) for d in range(1, N)]
    partners += [in_row(lax.rem(x + d, 4)) for d in range(1, 4)]
    partners += [in_quad(1 - p, y_hi), in_quad(p, 1 - y_hi), in_quad(1 - p, 1 - y_hi)]
    partners += [other_core, other_y]
    for partner in partners:
        pl.semaphore_signal(barrier, inc=1, device_id=partner, device_id_type=MESH)
    pl.semaphore_wait(barrier, len(partners))

    def remote(src, dst, send, recv, to):
        return pltpu.make_async_remote_copy(
            src_ref=src, dst_ref=dst, send_sem=send, recv_sem=recv, device_id=to, device_id_type=MESH
        )

    go_ring = Ring(go_b, go_rs, go_rr, z, in_ring, lambda h: p if h == 0 else 1 - p)
    ql_ring = Ring(ql_b, ql_rs, ql_rr, z, in_ring, lambda h: h)
    g_ring = Ring(g_b, g_rs, g_rr, z, in_ring, lambda h: h)
    n_ring = Ring(n_b, n_rs, n_rr, z, in_ring, lambda h: h)

    acts_load.wait()
    home = y_hi == p

    def acts_y(d):
        return remote(acts_v, acts_b.at[x, p], ya_send.at[d], ya_recv.at[p], in_quad(y_hi, d))

    for d in range(2):
        @pl.when(jnp.logical_not(jnp.logical_and(home, y_hi == d)))
        def _():
            acts_y(d).start()

    go_load.wait()
    go_swap = remote(go_b.at[z, p], go_b.at[z, p], gx_send, gx_recv, in_quad(1 - p, y_hi))
    go_swap.start()
    go_ring.start(0)

    @pl.when(home)
    def _():
        acts_b[x, p] = acts_v[...]

    def acts_y_in(p_):
        return remote(acts_v, acts_b.at[x, p_], ya_send.at[0], ya_recv.at[p_], in_quad(p, 0))

    for p_ in range(2):
        @pl.when(jnp.logical_not(jnp.logical_and(home, p == p_)))
        def _():
            acts_y_in(p_).wait_recv()

    def acts_x(d):
        return remote(acts_b.at[x], acts_b.at[x], xa_send.at[d - 1], xa_recv.at[d - 1], in_row(lax.rem(x + d, 4)))

    def acts_x_in(d):
        slot = lax.rem(x + 4 - d, 4)
        return remote(acts_b.at[slot], acts_b.at[slot], xa_send.at[d - 1], xa_recv.at[d - 1], in_row(slot))

    for d in (2, 1, 3):
        acts_x(d).start()

    remote(go_b.at[z, 1 - p], go_b.at[z, 1 - p], gx_send, gx_recv, in_quad(1 - p, y_hi)).wait_recv()
    go_ring.start(1)
    go_ring.forward(0, 0)

    def transpose_acts(x_):
        for h in range(2):
            at_v[lax.rem(x_, 2), lax.div(x_, 2), :, h * T : (h + 1) * T] = acts_b[x_, h].T

    transpose_acts(x)
    go_ring.forward(0, 1)
    go_ring.forward(1, 0)
    acts_x_in(1).wait_recv()
    transpose_acts(lax.rem(x + 3, 4))
    go_ring.forward(1, 1)
    go_ring.forward(2, 0)
    acts_x_in(3).wait_recv()
    transpose_acts(lax.rem(x + 1, 4))
    go_ring.forward(2, 1)

    for h in range(2):
        ql_load[h].wait()
        ql_ring.start(h)
    qr_load.wait()

    def qr_out(d):
        to = lax.rem(z + d, N)
        return remote(qr_v.at[:, lanes(to)], qrc.at[z], qr_send.at[d - 1], qr_recv.at[d - 1], in_ring(to))

    def qr_incoming(d):
        slot = lax.rem(z + N - d, N)
        return remote(qrc.at[slot], qrc.at[slot], qr_send.at[d - 1], qr_recv.at[d - 1], in_ring(slot))

    for d in (4, 3, 5, 2, 6, 1, 7):
        qr_out(d).start()

    acts_x_in(2).wait_recv()
    transpose_acts(lax.rem(x + 2, 4))
    go_ring.forward(3, 0)
    go_ring.forward(3, 1)

    def partial(which, dst):
        rows = at_v[which].reshape(2 * W, 2 * T)

        @pl.loop(0, N)
        def _(k):
            dst[:, :, lanes(k)] = dot_nn(rows, go_b[k].reshape(2 * T, W)).reshape(2, W, W)

    partial(1 - core, psend)

    def to_core(a_):
        return remote(psend.at[a_], d2d.at[a_], dd_send.at[a_], dd_recv.at[a_], other_core)

    to_core(1 - a).start()
    to_core(a).start()
    partial(core, pown)
    to_core(1 - a).wait_recv()

    def to_y(h):
        return remote(ysend.at[h], yrecv.at[h], yy_send.at[h], yy_recv.at[h], other_y)

    for h in range(2):
        rows = pl.ds(64 * h, 64)
        ysend[h] = (pown[1 - a, rows] + d2d[1 - a, rows]).astype(BF16)
        to_y(h).start()
    ql_ring.forward(0, 0)
    ql_ring.forward(0, 1)
    to_core(a).wait_recv()
    pown[a] = pown[a] + d2d[a]
    for h in range(2):
        rows = pl.ds(64 * h, 64)
        to_y(h).wait_recv()
        g_b[z, h] = (pown[a, rows] + yrecv[h].astype(F32)).astype(BF16)
        g_ring.start(h)
        ql_ring.forward(1, h)

    qrc[z] = qr_v[:, lanes(z)]
    qrct[:, lanes(z)] = qrc[z].T
    for d in range(1, N):
        qr_incoming(d).wait_recv()
        slot = lax.rem(z + N - d, N)
        qrct[:, lanes(slot)] = qrc[slot].T
    ql_ring.forward(2, 0)
    ql_ring.forward(2, 1)
    g_ring.forward(0, 0)
    for c in late_loads:
        c.wait()
    rf_v[...] = shampoo_beta * rf_v[...]

    def take_tile(k):
        tile = g_b[k].reshape(W, B)
        mixt[:, lanes(k)] = dot_nt(qrct[...], tile).astype(BF16)
        own = g_b[z].reshape(W, B)
        lf_v[:, lanes(k)] = shampoo_beta * lf_v[:, lanes(k)] + (1.0 - shampoo_beta) * dot_nt(own, tile)
        part = g_b[k, :, :, lanes(z)].reshape(W, W).T
        rf_v[...] = rf_v[...] + (1.0 - shampoo_beta) * dot_nn(part, tile)

    take_tile(z)
    g_ring.forward(0, 1)
    ql_ring.forward(3, 0)
    ql_ring.forward(3, 1)
    for s in range(3):
        if s > 0:
            g_ring.forward(s, 1)
        take_tile(lax.rem(z + N - 1 - s, N))
        g_ring.forward(s + 1, 0)
        take_tile(lax.rem(z + 1 + s, N))
    g_ring.forward(3, 1)
    take_tile(lax.rem(z + 4, N))

    for h in range(2):
        for t in range(2):
            first = h * 512 + t * 256
            basis = ql_b[:, :, :, first : first + 256].reshape(B, 256)
            rotated = dot_nn(mixt[...], basis).T
            rows = pl.ds(first, 256)
            first_new = first_beta * mo_v[rows] + (1.0 - first_beta) * rotated
            second_new = second_beta * se_v[rows] + (1.0 - second_beta) * rotated * rotated
            mo_v[rows] = first_new
            se_v[rows] = second_new
            normed = first_new / first_corr / (jnp.sqrt(second_new / second_corr) + epsilon)
            n_b[z, h, t * 256 : (t + 1) * 256] = normed.astype(BF16)
        n_ring.start(h)

    def store(src, dst, n):
        c = pltpu.make_async_copy(src, dst, store_sem.at[n])
        c.start()
        return c

    stores = [
        store(lf_v, lo_out.at[0], 0),
        store(rf_v, ro_out.at[0], 1),
        store(mo_v, mo_out, 2),
        store(se_v, se_out, 3),
    ]

    def take_steps(k, h, fresh=False):
        cols = slice(h * 512, (h + 1) * 512)
        term = dot_nt(qr_v[:, lanes(k)], n_b[k, h])
        back_v[:, cols] = term if fresh else back_v[:, cols] + term

    for h in range(2):
        take_steps(z, h, True)
    for s in range(3):
        for h in range(2):
            n_ring.forward(s, h)
            take_steps(lax.rem(z + N - 1 - s, N), h)
            take_steps(lax.rem(z + 1 + s, N), h)
    for h in range(2):
        n_ring.forward(3, h)
        take_steps(lax.rem(z + 4, N), h)

    back = back_v[...].astype(BF16)
    for k in range(N):
        up_v[k * W : (k + 1) * W] = dot_nt(ql_b[k].reshape(W, B), back).astype(BF16)
    stores.append(store(up_v, up_out, 4))

    for d in range(2):
        @pl.when(jnp.logical_not(jnp.logical_and(home, y_hi == d)))
        def _():
            acts_y(d).wait_send()

    go_swap.wait_send()
    for d in range(1, 4):
        acts_x(d).wait_send()
    for d in range(1, N):
        qr_out(d).wait_send()
    for a_ in (a, 1 - a):
        to_core(a_).wait_send()
    for h in range(2):
        to_y(h).wait_send()
    for ring in (go_ring, ql_ring, g_ring, n_ring):
        ring.finish()
    for c in stores:
        c.wait()


def shards(acts, grad_out, left_factor, right_factor, left_basis, right_basis, moment, second):
    anywhere = pl.BlockSpec(memory_space=pl.ANY)
    dma, vmem = pltpu.SemaphoreType.DMA, pltpu.VMEM
    ring = [dma((2, 4, 2)), dma((2, 4, 2))]
    return pl.pallas_call(
        kernel,
        out_shape=(
            jax.ShapeDtypeStruct(left_factor.shape, F32),
            jax.ShapeDtypeStruct(right_factor.shape, F32),
            jax.ShapeDtypeStruct(moment.shape, F32),
            jax.ShapeDtypeStruct(second.shape, F32),
            jax.ShapeDtypeStruct(moment.shape, BF16),
        ),
        in_specs=[anywhere] * 8,
        out_specs=[anywhere] * 5,
        scratch_shapes=[
            vmem((T, W), BF16),
            vmem((4, 2, T, W), BF16),
            vmem((2, 2, W, 2 * T), BF16),
            vmem((N, 2, T, W), BF16),
            vmem((2, W, B), F32),
            vmem((2, W, B), F32),
            vmem((2, W, B), F32),
            vmem((2, W // 2, B), BF16),
            vmem((2, W // 2, B), BF16),
            vmem((N, 2, W // 2, B), BF16),
            vmem((W, B), BF16),
            vmem((N, W, W), BF16),
            vmem((W, B), BF16),
            vmem((N, 2, W // 2, B), BF16),
            vmem((W, B), BF16),
            vmem((B, W), F32),
            vmem((B, W), F32),
            vmem((W, B), F32),
            vmem((W, B), F32),
            vmem((N, 2, B // 2, W), BF16),
            vmem((W, B), F32),
            vmem((B, W), BF16),
            dma((9,)),
            dma((5,)),
            dma((2,)), dma((2,)),
            dma((3,)), dma((3,)),
            dma, dma,
            dma((N - 1,)), dma((N - 1,)),
            dma((2,)), dma((2,)),
            dma((2,)), dma((2,)),
            *ring, *ring, *ring, *ring,
        ],
        compiler_params=pltpu.CompilerParams(
            collective_id=0, has_side_effects=True, vmem_limit_bytes=48 * 1024 * 1024
        ),
    )(acts, grad_out, left_factor, right_factor, left_basis, right_basis, moment, second)


def solution(mesh):
    by_tile, by_rows = P("tok", "col"), P("tok", "col", None)
    return jax.shard_map(
        shards,
        mesh=mesh,
        in_specs=(by_tile, by_tile, by_rows, by_rows, by_rows, by_rows, by_tile, by_tile),
        out_specs=(by_rows, by_rows, by_tile, by_tile, by_tile),
        check_vma=False,
    )
```

time: 490 us -> 122 us (0.25)
  the two profiles are of different devices: /device:TPU:9 before, /device:TPU:16 now
where the time goes in v1:
time: 122 us; the launch traced here: 121 us
  Pallas kernels  109 us (89%)
  local copies, waits for them, and re-layouts  11.6 us (10%)
    pallas_call x1, Pallas kernels, shards(): pl.pallas_call(kernel, out_shape=(jax.ShapeDtypeStruct(left_factor.shape,...  109 us
    unnamed x21, local copies, waits for them, and re-layouts  11.6 us

profile of v1, /device:TPU:16, one launch (start us, length us, event | category | flops | bytes accessed | tf_op | source)
XLA Modules:
  0.0 121.5 jit_solution(12059700362415972068)
XLA Ops:
  0.6 0.0 copy-start
  0.6 1.0 copy-done
  1.7 0.0 copy-start.1
  1.7 1.0 copy-done.1
  2.7 0.0 copy-start.2
  2.7 1.0 copy-done.2
  3.8 0.0 copy-start.3
  3.8 1.0 copy-done.3
  4.8 0.0 copy-start.4
  4.8 0.9 copy-done.4
  5.8 0.0 copy-start.5
  5.8 0.9 copy-done.5
  6.7 0.0 copy-start.6
  6.7 0.8 copy-done.6
  7.5 0.0 copy-start.7
  7.5 0.8 copy-done.7
  8.4 109.2 %shard_map.119 = (f32[1,128,1024]{2,1,0:T(8,128)S(1)}, f32[1,128,1024]{2,1,0:T(8,128)S(1)}, f32[1024,128]{1,0:T(8,128)S(1)}, f32[1024,128]{1,0:T(8,128)S(1)}, bf16[1024,128]{1,0:T(8,128)(2,1)S(1)}) custom-call(bf16[256,128]{1,0:T(8,128)(2,1)S(1)} %copy-done.6, bf16[256,128]{1,0:T(8,128)(2,1)S(1)} %copy-done.7, f32[1,128,1024]{2,1,0:T(8,128)S(1)} %copy-done, ...), custom_call_target="tpu_custom_call" | custom-call | tf_op jit(solution)/shard_map/pallas_call | solution.py:369
  117.6 0.8 copy.18
  118.4 0.8 copy.19
  119.2 0.8 copy.20
  120.0 0.8 copy.21
  120.8 0.7 copy.22
Async XLA Ops:
  0.6 1.0 copy-start
  1.7 1.0 copy-start.1
  2.7 1.0 copy-start.2
  3.8 1.0 copy-start.3
  4.8 0.9 copy-start.4
  5.8 0.9 copy-start.5
  6.7 0.8 copy-start.6
  7.5 0.8 copy-start.7

commit v2 on v1

v2 whole, which is shorter than its diff:
```python
import jax
import jax.numpy as jnp
from jax import lax
from jax.experimental import pallas as pl
from jax.experimental.pallas import tpu as pltpu
from jax.sharding import PartitionSpec as P

MESH = pl.DeviceIdType.MESH
F32 = jnp.float32
BF16 = jnp.bfloat16

shampoo_beta = 0.95
first_beta = 0.9
second_beta = 0.95
first_corr = 1.0 - 0.9**4
second_corr = 1.0 - 0.95**4
epsilon = 1e-08

B = 1024
W = 128
T = 256
HALF = B // 2
N = 8


def dot_nn(a, b):
    return lax.dot_general(a, b, (((1,), (0,)), ((), ())), preferred_element_type=F32)


def dot_nt(a, b):
    return lax.dot_general(a, b, (((1,), (1,)), ((), ())), preferred_element_type=F32)


def lanes(k, size=W):
    return pl.ds(pl.multiple_of(k * size, size), size)


class Ring:
    def __init__(self, buf, send, recv, z, at, half):
        self.buf, self.send, self.recv, self.z, self.at, self.half = buf, send, recv, z, at, half

    @staticmethod
    def valid(s, h, way):
        return s < 3 or h == way

    def copy(self, s, h, way, slot, to):
        ref = self.buf.at[slot, self.half(h)]
        return pltpu.make_async_remote_copy(
            src_ref=ref,
            dst_ref=ref,
            send_sem=self.send.at[way, s, h],
            recv_sem=self.recv.at[way, s, h],
            device_id=self.at(to),
            device_id_type=MESH,
        )

    def outgoing(self, s, h, way):
        slot = lax.rem(self.z + (N - s if way == 0 else s), N)
        to = lax.rem(self.z + (1 if way == 0 else N - 1), N)
        return self.copy(s, h, way, slot, to)

    def incoming(self, s, h, way):
        slot = lax.rem(self.z + (N - 1 - s if way == 0 else 1 + s), N)
        to = lax.rem(self.z + (1 if way == 0 else N - 1), N)
        return self.copy(s, h, way, slot, to)

    def start(self, h):
        for way in range(2):
            self.outgoing(0, h, way).start()

    def forward(self, s, h):
        for way in range(2):
            if self.valid(s, h, way):
                self.incoming(s, h, way).wait_recv()
                if s < 3 and self.valid(s + 1, h, way):
                    self.outgoing(s + 1, h, way).start()

    def finish(self):
        for s in range(4):
            for h in range(2):
                for way in range(2):
                    if self.valid(s, h, way):
                        self.outgoing(s, h, way).wait_send()


def kernel(
    acts_in, go_in, lf_in, rf_in, ql_in, qr_in, mo_in, se_in,
    lf_v, rf_v, mo_v, se_v, back_v, ql_b,
    acts_v, acts_b, at_v, go_b, psend, pown, d2d, ysend, yrecv,
    qr_v, qrc, qrct, g_b, mixt, n_b, sums,
    load_sem,
    ya_send, ya_recv, xa_send, xa_recv, gx_send, gx_recv, qr_send, qr_recv,
    dd_send, dd_recv, yy_send, yy_recv,
    go_rs, go_rr, ql_rs, ql_rr, g_rs, g_rr, n_rs, n_rr,
):
    tok, col = lax.axis_index("tok"), lax.axis_index("col")
    z, blk = lax.rem(col, N), lax.div(col, N)
    y_hi, x = lax.div(blk, 4), lax.rem(blk, 4)
    p, q = lax.div(tok, 4), lax.rem(tok, 4)
    a, core = lax.div(q, 2), lax.rem(q, 2)

    def dev(col_, tok_):
        return {"col": col_, "tok": tok_}

    def in_ring(z_):
        return dev(blk * N + z_, tok)

    def in_quad(p_, y_hi_):
        return dev((y_hi_ * 4 + x) * N + z, p_ * 4 + q)

    def in_row(x_):
        return dev((y_hi * 4 + x_) * N + z, tok)

    other_core = dev(col, p * 4 + a * 2 + 1 - core)
    other_y = dev(col, p * 4 + (1 - a) * 2 + core)

    def load(src, dst, n):
        c = pltpu.make_async_copy(src, dst, load_sem.at[n])
        c.start()
        return c

    go_load = load(go_in, go_b.at[z, p], 0)
    acts_load = load(acts_in, acts_v, 1)
    ql_load = [load(ql_in.at[0, :, pl.ds(HALF * h, HALF)], ql_b.at[z, h], 2 + h) for h in range(2)]
    qr_load = load(qr_in.at[0], qr_v, 4)
    late_loads = [
        load(mo_in, mo_v, 5),
        load(se_in, se_v, 6),
        load(lf_in.at[0], lf_v, 7),
        load(rf_in.at[0], rf_v, 8),
    ]

    barrier = pltpu.get_barrier_semaphore()
    partners = [in_ring(lax.rem(z + d, N)) for d in range(1, N)]
    partners += [in_row(lax.rem(x + d, 4)) for d in range(1, 4)]
    partners += [in_quad(1 - p, y_hi), in_quad(p, 1 - y_hi), in_quad(1 - p, 1 - y_hi)]
    partners += [other_core, other_y]
    for partner in partners:
        pl.semaphore_signal(barrier, inc=1, device_id=partner, device_id_type=MESH)
    pl.semaphore_wait(barrier, len(partners))

    def remote(src, dst, send, recv, to):
        return pltpu.make_async_remote_copy(
            src_ref=src, dst_ref=dst, send_sem=send, recv_sem=recv, device_id=to, device_id_type=MESH
        )

    go_ring = Ring(go_b, go_rs, go_rr, z, in_ring, lambda h: p if h == 0 else 1 - p)
    ql_ring = Ring(ql_b, ql_rs, ql_rr, z, in_ring, lambda h: h)
    g_ring = Ring(g_b, g_rs, g_rr, z, in_ring, lambda h: h)
    n_ring = Ring(n_b, n_rs, n_rr, z, in_ring, lambda h: h)

    go_load.wait()
    go_ring.start(0)
    go_swap = remote(go_b.at[z, p], go_b.at[z, p], gx_send, gx_recv, in_quad(1 - p, y_hi))
    go_swap.start()

    acts_load.wait()
    home = y_hi == p

    def acts_y(d):
        return remote(acts_v, acts_b.at[x, p], ya_send.at[d], ya_recv.at[p], in_quad(y_hi, d))

    for d in range(2):
        @pl.when(jnp.logical_not(jnp.logical_and(home, y_hi == d)))
        def _():
            acts_y(d).start()

    ql_load[0].wait()
    ql_ring.start(0)

    @pl.when(home)
    def _():
        acts_b[x, p] = acts_v[...]

    remote(go_b.at[z, 1 - p], go_b.at[z, 1 - p], gx_send, gx_recv, in_quad(1 - p, y_hi)).wait_recv()
    go_ring.start(1)
    go_ring.forward(0, 0)

    def acts_y_in(p_):
        return remote(acts_v, acts_b.at[x, p_], ya_send.at[0], ya_recv.at[p_], in_quad(p, 0))

    for p_ in range(2):
        @pl.when(jnp.logical_not(jnp.logical_and(home, p == p_)))
        def _():
            acts_y_in(p_).wait_recv()

    def acts_x(d):
        return remote(acts_b.at[x], acts_b.at[x], xa_send.at[d - 1], xa_recv.at[d - 1], in_row(lax.rem(x + d, 4)))

    def acts_x_in(d):
        slot = lax.rem(x + 4 - d, 4)
        return remote(acts_b.at[slot], acts_b.at[slot], xa_send.at[d - 1], xa_recv.at[d - 1], in_row(slot))

    for d in (2, 1, 3):
        acts_x(d).start()

    qr_load.wait()

    def qr_out(d):
        to = lax.rem(z + d, N)
        return remote(qr_v.at[:, lanes(to)], qrc.at[z], qr_send.at[d - 1], qr_recv.at[d - 1], in_ring(to))

    def qr_incoming(d):
        slot = lax.rem(z + N - d, N)
        return remote(qrc.at[slot], qrc.at[slot], qr_send.at[d - 1], qr_recv.at[d - 1], in_ring(slot))

    def transpose_acts(x_):
        for h in range(2):
            at_v[lax.rem(x_, 2), lax.div(x_, 2), :, h * T : (h + 1) * T] = acts_b[x_, h].T

    for d in (4, 3, 5):
        qr_out(d).start()
    go_ring.forward(0, 1)
    go_ring.forward(1, 0)
    transpose_acts(x)
    ql_ring.forward(0, 0)
    go_ring.forward(1, 1)
    for d in (2, 6, 1, 7):
        qr_out(d).start()
    go_ring.forward(2, 0)
    acts_x_in(1).wait_recv()
    transpose_acts(lax.rem(x + 3, 4))
    go_ring.forward(2, 1)
    acts_x_in(3).wait_recv()
    transpose_acts(lax.rem(x + 1, 4))
    acts_x_in(2).wait_recv()
    transpose_acts(lax.rem(x + 2, 4))

    def chunk(place):
        ahead, step = lax.rem(place, 2), lax.div(place + 1, 2)
        return lax.rem(z + ahead * step + (1 - ahead) * (N - step), N)

    groups = (slice(0, 5), slice(5, 8))

    def partial(group):
        @pl.loop(group.start, group.stop)
        def _(place):
            part = go_b[chunk(place)].reshape(2 * T, W)
            psend[:, place] = dot_nn(at_v[1 - core].reshape(2 * W, 2 * T), part).reshape(2, W, W)
            pown[:, place] = dot_nn(at_v[core].reshape(2 * W, 2 * T), part).reshape(2, W, W)

    def to_core(n, a_):
        span = pl.ds(groups[n].start, groups[n].stop - groups[n].start)
        return remote(psend.at[a_, span], d2d.at[a_, span], dd_send.at[n, a_], dd_recv.at[n, a_], other_core)

    def to_y(n):
        span = pl.ds(groups[n].start, groups[n].stop - groups[n].start)
        return remote(ysend.at[span], yrecv.at[span], yy_send.at[n], yy_recv.at[n], other_y)

    def send_y(n):
        to_core(n, 1 - a).wait_recv()
        for place in range(groups[n].start, groups[n].stop):
            ysend[place] = (pown[1 - a, place] + d2d[1 - a, place]).astype(BF16)
        to_y(n).start()

    def take_y(n):
        to_core(n, a).wait_recv()
        to_y(n).wait_recv()
        for place in range(groups[n].start, groups[n].stop):
            tile = (pown[a, place] + d2d[a, place] + yrecv[place].astype(F32)).astype(BF16)
            g_b[z, :, :, lanes(chunk(place))] = tile.reshape(2, W // 2, W)

    partial(groups[0])
    to_core(0, 1 - a).start()
    to_core(0, a).start()
    go_ring.forward(3, 0)
    go_ring.forward(3, 1)
    ql_ring.forward(1, 0)
    partial(groups[1])
    to_core(1, 1 - a).start()
    to_core(1, a).start()
    send_y(0)
    send_y(1)
    ql_ring.forward(2, 0)

    qrc[z] = qr_v[:, lanes(z)]
    qrct[:, lanes(z)] = qrc[z].T
    for d in range(1, N):
        qr_incoming(d).wait_recv()
        slot = lax.rem(z + N - d, N)
        qrct[:, lanes(slot)] = qrc[slot].T

    take_y(0)
    take_y(1)
    for h in range(2):
        g_ring.start(h)

    def mix(k):
        mixt[:, lanes(k)] = dot_nt(qrct[...], g_b[k].reshape(W, B)).astype(BF16)

    mix(z)
    ql_ring.forward(3, 0)
    for s in range(3):
        g_ring.forward(s, 0)
        g_ring.forward(s, 1)
        if s == 0:
            ql_load[1].wait()
            ql_ring.start(1)
        else:
            ql_ring.forward(s - 1, 1)
        mix(lax.rem(z + N - 1 - s, N))
        mix(lax.rem(z + 1 + s, N))
    g_ring.forward(3, 0)
    g_ring.forward(3, 1)
    mix(lax.rem(z + 4, N))
    for c in late_loads:
        c.wait()

    def rotate(h):
        for t in range(2):
            basis = ql_b[:, h, :, t * 256 : (t + 1) * 256].reshape(B, 256)
            rotated = dot_nn(mixt[...], basis).T
            rows = pl.ds(h * HALF + t * 256, 256)
            first_new = first_beta * mo_v[rows] + (1.0 - first_beta) * rotated
            second_new = second_beta * se_v[rows] + (1.0 - second_beta) * rotated * rotated
            mo_v[rows] = first_new
            se_v[rows] = second_new
            normed = first_new / first_corr / (jnp.sqrt(second_new / second_corr) + epsilon)
            n_b[z, h, t * 256 : (t + 1) * 256] = normed.astype(BF16)
        n_ring.start(h)

    def factors(k):
        tile = g_b[k].reshape(W, B)
        lf_v[:, lanes(k)] = shampoo_beta * lf_v[:, lanes(k)] + (1.0 - shampoo_beta) * dot_nt(g_b[z].reshape(W, B), tile)
        part = g_b[k, :, :, lanes(z)].reshape(W, W).T
        rf_v[...] = rf_v[...] + (1.0 - shampoo_beta) * dot_nn(part, tile)

    def take_steps(k, h, fresh=False):
        cols = slice(h * HALF, (h + 1) * HALF)
        term = dot_nt(qr_v[:, lanes(k)], n_b[k, h])
        sums[:, cols] = term if fresh else sums[:, cols] + term

    rotate(0)
    ql_ring.forward(2, 1)
    rf_v[...] = shampoo_beta * rf_v[...]
    take_steps(z, 0, True)
    ql_ring.forward(3, 1)
    rotate(1)
    take_steps(z, 1, True)
    for s in range(3):
        for h in range(2):
            n_ring.forward(s, h)
            take_steps(lax.rem(z + N - 1 - s, N), h)
            take_steps(lax.rem(z + 1 + s, N), h)
            factors(lax.rem(z + 2 * s + h, N))
    factors(lax.rem(z + 6, N))
    factors(lax.rem(z + 7, N))
    for h in range(2):
        n_ring.forward(3, h)
        take_steps(lax.rem(z + 4, N), h)
    back_v[...] = sums[...].astype(BF16)

    for d in range(2):
        @pl.when(jnp.logical_not(jnp.logical_and(home, y_hi == d)))
        def _():
            acts_y(d).wait_send()

    go_swap.wait_send()
    for d in range(1, 4):
        acts_x(d).wait_send()
    for d in range(1, N):
        qr_out(d).wait_send()
    for n in range(2):
        for a_ in (a, 1 - a):
            to_core(n, a_).wait_send()
        to_y(n).wait_send()
    for ring in (go_ring, ql_ring, g_ring, n_ring):
        ring.finish()


def finish(lf_v, rf_v, mo_v, se_v, back_v, ql_b, lo_out, ro_out, mo_out, se_out, up_out, up_v, store_sem):
    def store(src, dst, n):
        c = pltpu.make_async_copy(src, dst, store_sem.at[n])
        c.start()
        return c

    stores = [
        store(lf_v, lo_out.at[0], 0),
        store(rf_v, ro_out.at[0], 1),
        store(mo_v, mo_out, 2),
        store(se_v, se_out, 3),
    ]
    for k in range(N):
        total = dot_nt(ql_b[k, 0], back_v[:, :HALF]) + dot_nt(ql_b[k, 1], back_v[:, HALF:])
        up_v[k * W : (k + 1) * W] = total.astype(BF16)
    stores.append(store(up_v, up_out, 4))
    for c in stores:
        c.wait()


def shards(acts, grad_out, left_factor, right_factor, left_basis, right_basis, moment, second):
    dma, vmem = pltpu.SemaphoreType.DMA, pltpu.VMEM
    hbm, on_chip = pl.BlockSpec(memory_space=pltpu.HBM), pl.BlockSpec(memory_space=pltpu.VMEM)
    ring = [dma((2, 4, 2)), dma((2, 4, 2))]
    arrays = (acts, grad_out, left_factor, right_factor, left_basis, right_basis, moment, second)
    shape = jax.ShapeDtypeStruct
    held = pl.pallas_call(
        kernel,
        out_shape=(
            shape((W, B), F32),
            shape((W, B), F32),
            shape((B, W), F32),
            shape((B, W), F32),
            shape((W, B), BF16),
            shape((N, 2, W, HALF), BF16),
        ),
        in_specs=[hbm] * 8,
        out_specs=[on_chip] * 6,
        scratch_shapes=[
            vmem((T, W), BF16),
            vmem((4, 2, T, W), BF16),
            vmem((2, 2, W, 2 * T), BF16),
            vmem((N, 2, T, W), BF16),
            vmem((2, N, W, W), F32),
            vmem((2, N, W, W), F32),
            vmem((2, N, W, W), F32),
            vmem((N, W, W), BF16),
            vmem((N, W, W), BF16),
            vmem((W, B), BF16),
            vmem((N, W, W), BF16),
            vmem((W, B), BF16),
            vmem((N, 2, W // 2, B), BF16),
            vmem((W, B), BF16),
            vmem((N, 2, HALF, W), BF16),
            vmem((W, B), F32),
            dma((9,)),
            dma((2,)), dma((2,)),
            dma((3,)), dma((3,)),
            dma, dma,
            dma((N - 1,)), dma((N - 1,)),
            dma((2, 2)), dma((2, 2)),
            dma((2,)), dma((2,)),
            *ring, *ring, *ring, *ring,
        ],
        compiler_params=pltpu.CompilerParams(
            collective_id=0, has_side_effects=True, vmem_limit_bytes=40 * 1024 * 1024
        ),
    )(*(pltpu.with_memory_space_constraint(v, pltpu.HBM) for v in arrays))
    return pl.pallas_call(
        finish,
        out_shape=(
            shape(left_factor.shape, F32),
            shape(right_factor.shape, F32),
            shape(moment.shape, F32),
            shape(second.shape, F32),
            shape(moment.shape, BF16),
        ),
        in_specs=[on_chip] * 6,
        out_specs=[hbm] * 5,
        scratch_shapes=[vmem((B, W), BF16), dma((5,))],
        compiler_params=pltpu.CompilerParams(vmem_limit_bytes=16 * 1024 * 1024),
    )(*held)


def solution(mesh):
    by_tile, by_rows = P("tok", "col"), P("tok", "col", None)
    return jax.shard_map(
        shards,
        mesh=mesh,
        in_specs=(by_tile, by_tile, by_rows, by_rows, by_rows, by_rows, by_tile, by_tile),
        out_specs=(by_rows, by_rows, by_tile, by_tile, by_tile),
        check_vma=False,
    )
```

time: 122 us -> 109 us (0.89)
  the two profiles are of different devices: /device:TPU:16 before, /device:TPU:12 now
where the time goes in v2:
time: 109 us
  Pallas kernels  109 us (100%)
    pallas_call x1, Pallas kernels, shards(): pl.pallas_call(kernel, out_shape=(shape((W, B), F32), shape((W, B), F32),...  107 us

profile of v2, /device:TPU:12, one launch (start us, length us, event | category | flops | bytes accessed | tf_op | source)
XLA Modules:
  0.0 109.3 jit_solution(13404621109534030017)
XLA Ops:
  0.6 107.0 %shard_map.119 = (f32[128,1024]{1,0:T(8,128)S(1)}, f32[128,1024]{1,0:T(8,128)S(1)}, f32[1024,128]{1,0:T(8,128)S(1)}, f32[1024,128]{1,0:T(8,128)S(1)}, bf16[128,1...) custom-call(bf16[256,128]{1,0:T(8,128)(2,1)} %acts_in.1, bf16[256,128]{1,0:T(8,128)(2,1)} %go_in.1, ...), custom_call_target="tpu_custom_call" | custom-call | tf_op jit(solution)/shard_map/pallas_call | solution.py:397
  107.7 1.7 %shard_map.120 = (f32[1,128,1024]{2,1,0:T(8,128)}, f32[1,128,1024]{2,1,0:T(8,128)}, f32[1024,128]{1,0:T(8,128)}, f32[1024,128]{1,0:T(8,128)}, bf16[1024,128]{1,0:T(8,128)(2,1)}) custom-call(f32[128,1024]{1,0:T(8,128)S(1)} %get-tuple-element.11.lf_v, f32[128,1024]{1,0:T(8,128)S(1)} %get-tuple-element.12.rf_v, f32[1024,128]{1,0:T(8,128)S(1)} %get-tuple-element.13.mo_v, ...), custom_call_target="tpu_custom_call" | custom-call | tf_op jit(solution)/shard_map/pallas_call | solution.py:439

commit v3 on v2

--- a/solution.py
+++ b/solution.py
@@ -36,15 +36,15 @@
 
 
 class Ring:
-    def __init__(self, buf, send, recv, z, at, half):
-        self.buf, self.send, self.recv, self.z, self.at, self.half = buf, send, recv, z, at, half
-
-    @staticmethod
-    def valid(s, h, way):
-        return s < 3 or h == way
+    def __init__(self, buf, send, recv, z, at, place=lambda h: h):
+        self.buf, self.send, self.recv, self.z, self.at, self.place = buf, send, recv, z, at, place
+        self.pieces = buf.shape[1]
+
+    def ways(self, s, h):
+        return (0, 1) if s < 3 else (0,) if 2 * h < self.pieces else (1,)
 
     def copy(self, s, h, way, slot, to):
-        ref = self.buf.at[slot, self.half(h)]
+        ref = self.buf.at[slot, self.place(h)]
         return pltpu.make_async_remote_copy(
             src_ref=ref,
             dst_ref=ref,
@@ -65,28 +65,26 @@
         return self.copy(s, h, way, slot, to)
 
     def start(self, h):
-        for way in range(2):
+        for way in (0, 1):
             self.outgoing(0, h, way).start()
 
     def forward(self, s, h):
-        for way in range(2):
-            if self.valid(s, h, way):
-                self.incoming(s, h, way).wait_recv()
-                if s < 3 and self.valid(s + 1, h, way):
-                    self.outgoing(s + 1, h, way).start()
+        for way in self.ways(s, h):
+            self.incoming(s, h, way).wait_recv()
+            if s < 3 and way in self.ways(s + 1, h):
+                self.outgoing(s + 1, h, way).start()
 
     def finish(self):
         for s in range(4):
-            for h in range(2):
-                for way in range(2):
-                    if self.valid(s, h, way):
-                        self.outgoing(s, h, way).wait_send()
+            for h in range(self.pieces):
+                for way in self.ways(s, h):
+                    self.outgoing(s, h, way).wait_send()
 
 
 def kernel(
     acts_in, go_in, lf_in, rf_in, ql_in, qr_in, mo_in, se_in,
     lf_v, rf_v, mo_v, se_v, back_v, ql_b,
-    acts_v, acts_b, at_v, go_b, psend, pown, d2d, ysend, yrecv,
+    acts_v, relay, acts_b, at_v, go_b, psend, pown, d2d, ysend, yrecv,
     qr_v, qrc, qrct, g_b, mixt, n_b, sums,
     load_sem,
     ya_send, ya_recv, xa_send, xa_recv, gx_send, gx_recv, qr_send, qr_recv,
@@ -145,9 +143,9 @@
         )
 
     go_ring = Ring(go_b, go_rs, go_rr, z, in_ring, lambda h: p if h == 0 else 1 - p)
-    ql_ring = Ring(ql_b, ql_rs, ql_rr, z, in_ring, lambda h: h)
-    g_ring = Ring(g_b, g_rs, g_rr, z, in_ring, lambda h: h)
-    n_ring = Ring(n_b, n_rs, n_rr, z, in_ring, lambda h: h)
+    ql_ring = Ring(ql_b, ql_rs, ql_rr, z, in_ring)
+    g_ring = Ring(g_b, g_rs, g_rr, z, in_ring)
+    n_ring = Ring(n_b, n_rs, n_rr, z, in_ring)
 
     go_load.wait()
     go_ring.start(0)
@@ -156,14 +154,40 @@
 
     acts_load.wait()
     home = y_hi == p
+    last = jnp.logical_and(p == 1, y_hi == 1)
+    third = jnp.logical_and(p == 0, y_hi == 1)
 
     def acts_y(d):
         return remote(acts_v, acts_b.at[x, p], ya_send.at[d], ya_recv.at[p], in_quad(y_hi, d))
 
+    def acts_back():
+        return remote(acts_v, relay, ya_send.at[0], ya_recv.at[2], in_quad(0, 1))
+
+    def acts_relay():
+        return remote(relay, acts_b.at[x, 1], ya_send.at[2], ya_recv.at[1], in_quad(1, 0))
+
+    def direct(d):
+        same = jnp.logical_and(home, y_hi == d)
+        return jnp.logical_not(jnp.logical_or(same, last) if d == 0 else same)
+
     for d in range(2):
-        @pl.when(jnp.logical_not(jnp.logical_and(home, y_hi == d)))
+        @pl.when(direct(d))
         def _():
             acts_y(d).start()
+
+    @pl.when(last)
+    def _():
+        acts_back().start()
+
+    qr_load.wait()
+
+    def qr_out(d):
+        to = lax.rem(z + d, N)
+        return remote(qr_v.at[:, lanes(to)], qrc.at[z], qr_send.at[d - 1], qr_recv.at[d - 1], in_ring(to))
+
+    def qr_incoming(d):
+        slot = lax.rem(z + N - d, N)
+        return remote(qrc.at[slot], qrc.at[slot], qr_send.at[d - 1], qr_recv.at[d - 1], in_ring(slot))
 
     ql_load[0].wait()
     ql_ring.start(0)
@@ -172,80 +196,97 @@
     def _():
         acts_b[x, p] = acts_v[...]
 
+    def acts_y_in(p_):
+        return remote(acts_v, acts_b.at[x, p_], ya_send.at[0], ya_recv.at[p_], in_quad(p, 0))
+
+    right, left = lax.rem(x + 1, 4), lax.rem(x + 3, 4)
+
+    def acts_x(n, kind, x_, to):
+        ref = acts_b.at[x_, y_hi if n == 0 else 1 - y_hi]
+        return remote(ref, ref, xa_send.at[n, kind], xa_recv.at[n, kind], in_row(to))
+
+    def acts_x_out(n, kind):
+        if kind < 2:
+            return acts_x(n, kind, x, (right, left)[kind])
+        return acts_x(n, 2, left, right) if n == 0 else acts_x(n, 2, right, left)
+
+    def acts_x_slot(kind):
+        return (left, right, lax.rem(x + 2, 4))[kind]
+
+    def acts_x_in(n, kind):
+        return acts_x(n, kind, acts_x_slot(kind), right)
+
+    def transpose_acts(n, x_):
+        p_ = y_hi if n == 0 else 1 - y_hi
+        at_v[lax.rem(x_, 2), lax.div(x_, 2), :, lanes(p_, T)] = acts_b[x_, p_].T
+
+    @pl.when(jnp.logical_not(home))
+    def _():
+        acts_y_in(y_hi).wait_recv()
+
+    for kind in range(2):
+        acts_x_out(0, kind).start()
+    go_ring.forward(0, 0)
     remote(go_b.at[z, 1 - p], go_b.at[z, 1 - p], gx_send, gx_recv, in_quad(1 - p, y_hi)).wait_recv()
     go_ring.start(1)
-    go_ring.forward(0, 0)
-
-    def acts_y_in(p_):
-        return remote(acts_v, acts_b.at[x, p_], ya_send.at[0], ya_recv.at[p_], in_quad(p, 0))
-
-    for p_ in range(2):
-        @pl.when(jnp.logical_not(jnp.logical_and(home, p == p_)))
-        def _():
-            acts_y_in(p_).wait_recv()
-
-    def acts_x(d):
-        return remote(acts_b.at[x], acts_b.at[x], xa_send.at[d - 1], xa_recv.at[d - 1], in_row(lax.rem(x + d, 4)))
-
-    def acts_x_in(d):
-        slot = lax.rem(x + 4 - d, 4)
-        return remote(acts_b.at[slot], acts_b.at[slot], xa_send.at[d - 1], xa_recv.at[d - 1], in_row(slot))
-
-    for d in (2, 1, 3):
-        acts_x(d).start()
-
-    qr_load.wait()
-
-    def qr_out(d):
-        to = lax.rem(z + d, N)
-        return remote(qr_v.at[:, lanes(to)], qrc.at[z], qr_send.at[d - 1], qr_recv.at[d - 1], in_ring(to))
-
-    def qr_incoming(d):
-        slot = lax.rem(z + N - d, N)
-        return remote(qrc.at[slot], qrc.at[slot], qr_send.at[d - 1], qr_recv.at[d - 1], in_ring(slot))
-
-    def transpose_acts(x_):
-        for h in range(2):
-            at_v[lax.rem(x_, 2), lax.div(x_, 2), :, h * T : (h + 1) * T] = acts_b[x_, h].T
-
-    for d in (4, 3, 5):
-        qr_out(d).start()
+
+    @pl.when(third)
+    def _():
+        acts_back().wait_recv()
+        acts_relay().start()
+
+    acts_x_in(0, 0).wait_recv()
+    acts_x_out(0, 2).start()
+    go_ring.forward(1, 0)
+    ql_ring.forward(0, 0)
+    acts_y_in(1 - y_hi).wait_recv()
+    for kind in range(2):
+        acts_x_out(1, kind).start()
     go_ring.forward(0, 1)
-    go_ring.forward(1, 0)
-    transpose_acts(x)
-    ql_ring.forward(0, 0)
+    for n in range(2):
+        transpose_acts(n, x)
+    transpose_acts(0, left)
+    acts_x_in(0, 1).wait_recv()
+    transpose_acts(0, right)
+    go_ring.forward(2, 0)
+    acts_x_in(1, 1).wait_recv()
+    acts_x_out(1, 2).start()
     go_ring.forward(1, 1)
-    for d in (2, 6, 1, 7):
-        qr_out(d).start()
-    go_ring.forward(2, 0)
-    acts_x_in(1).wait_recv()
-    transpose_acts(lax.rem(x + 3, 4))
-    go_ring.forward(2, 1)
-    acts_x_in(3).wait_recv()
-    transpose_acts(lax.rem(x + 1, 4))
-    acts_x_in(2).wait_recv()
-    transpose_acts(lax.rem(x + 2, 4))
+    ql_ring.forward(1, 0)
+    ql_load[1].wait()
+    ql_ring.start(1)
+    transpose_acts(1, right)
+    acts_x_in(1, 0).wait_recv()
+    transpose_acts(1, left)
+    for n in range(2):
+        acts_x_in(n, 2).wait_recv()
+        transpose_acts(n, acts_x_slot(2))
+    go_ring.forward(3, 0)
 
     def chunk(place):
         ahead, step = lax.rem(place, 2), lax.div(place + 1, 2)
         return lax.rem(z + ahead * step + (1 - ahead) * (N - step), N)
 
-    groups = (slice(0, 5), slice(5, 8))
-
-    def partial(group):
-        @pl.loop(group.start, group.stop)
+    groups = (slice(0, 5), slice(5, 7), slice(7, 8))
+
+    def span(n):
+        return pl.ds(groups[n].start, groups[n].stop - groups[n].start)
+
+    def partial(n):
+        @pl.loop(groups[n].start, groups[n].stop)
         def _(place):
             part = go_b[chunk(place)].reshape(2 * T, W)
             psend[:, place] = dot_nn(at_v[1 - core].reshape(2 * W, 2 * T), part).reshape(2, W, W)
             pown[:, place] = dot_nn(at_v[core].reshape(2 * W, 2 * T), part).reshape(2, W, W)
 
+        for a_ in (1 - a, a):
+            to_core(n, a_).start()
+
     def to_core(n, a_):
-        span = pl.ds(groups[n].start, groups[n].stop - groups[n].start)
-        return remote(psend.at[a_, span], d2d.at[a_, span], dd_send.at[n, a_], dd_recv.at[n, a_], other_core)
+        return remote(psend.at[a_, span(n)], d2d.at[a_, span(n)], dd_send.at[n, a_], dd_recv.at[n, a_], other_core)
 
     def to_y(n):
-        span = pl.ds(groups[n].start, groups[n].stop - groups[n].start)
-        return remote(ysend.at[span], yrecv.at[span], yy_send.at[n], yy_recv.at[n], other_y)
+        return remote(ysend.at[span(n)], yrecv.at[span(n)], yy_send.at[n], yy_recv.at[n], other_y)
 
     def send_y(n):
         to_core(n, 1 - a).wait_recv()
@@ -258,20 +299,28 @@
         to_y(n).wait_recv()
         for place in range(groups[n].start, groups[n].stop):
             tile = (pown[a, place] + d2d[a, place] + yrecv[place].astype(F32)).astype(BF16)
-            g_b[z, :, :, lanes(chunk(place))] = tile.reshape(2, W // 2, W)
-
-    partial(groups[0])
-    to_core(0, 1 - a).start()
-    to_core(0, a).start()
-    go_ring.forward(3, 0)
+            g_b[z, :, :, lanes(chunk(place))] = tile.reshape(4, W // 4, W)
+
+    partial(0)
+    go_ring.forward(2, 1)
+    ql_ring.forward(2, 0)
+    partial(1)
+    send_y(0)
+    for d in (1, 7, 2, 6):
+        qr_out(d).start()
+    ql_ring.forward(0, 1)
     go_ring.forward(3, 1)
-    ql_ring.forward(1, 0)
-    partial(groups[1])
-    to_core(1, 1 - a).start()
-    to_core(1, a).start()
-    send_y(0)
+    partial(2)
     send_y(1)
-    ql_ring.forward(2, 0)
+    send_y(2)
+    for d in (3, 5, 4):
+        qr_out(d).start()
+    ql_ring.forward(3, 0)
+    ql_ring.forward(1, 1)
+    for n in range(3):
+        take_y(n)
+    for h in range(4):
+        g_ring.start(h)
 
     qrc[z] = qr_v[:, lanes(z)]
     qrct[:, lanes(z)] = qrc[z].T
@@ -280,43 +329,33 @@
         slot = lax.rem(z + N - d, N)
         qrct[:, lanes(slot)] = qrc[slot].T
 
-    take_y(0)
-    take_y(1)
-    for h in range(2):
-        g_ring.start(h)
-
     def mix(k):
         mixt[:, lanes(k)] = dot_nt(qrct[...], g_b[k].reshape(W, B)).astype(BF16)
 
     mix(z)
-    ql_ring.forward(3, 0)
     for s in range(3):
-        g_ring.forward(s, 0)
-        g_ring.forward(s, 1)
-        if s == 0:
-            ql_load[1].wait()
-            ql_ring.start(1)
-        else:
-            ql_ring.forward(s - 1, 1)
+        for h in range(4):
+            g_ring.forward(s, h)
+        if s < 2:
+            ql_ring.forward(2 + s, 1)
         mix(lax.rem(z + N - 1 - s, N))
         mix(lax.rem(z + 1 + s, N))
-    g_ring.forward(3, 0)
-    g_ring.forward(3, 1)
+    for h in range(4):
+        g_ring.forward(3, h)
     mix(lax.rem(z + 4, N))
     for c in late_loads:
         c.wait()
 
     def rotate(h):
-        for t in range(2):
-            basis = ql_b[:, h, :, t * 256 : (t + 1) * 256].reshape(B, 256)
-            rotated = dot_nn(mixt[...], basis).T
-            rows = pl.ds(h * HALF + t * 256, 256)
-            first_new = first_beta * mo_v[rows] + (1.0 - first_beta) * rotated
-            second_new = second_beta * se_v[rows] + (1.0 - second_beta) * rotated * rotated
-            mo_v[rows] = first_new
-            se_v[rows] = second_new
-            normed = first_new / first_corr / (jnp.sqrt(second_new / second_corr) + epsilon)
-            n_b[z, h, t * 256 : (t + 1) * 256] = normed.astype(BF16)
+        basis = ql_b[:, h // 2, :, (h % 2) * 256 : (h % 2 + 1) * 256].reshape(B, 256)
+        rotated = dot_nn(mixt[...], basis).T
+        rows = pl.ds(h * 256, 256)
+        first_new = first_beta * mo_v[rows] + (1.0 - first_beta) * rotated
+        second_new = second_beta * se_v[rows] + (1.0 - second_beta) * rotated * rotated
+        mo_v[rows] = first_new
+        se_v[rows] = second_new
+        normed = first_new / first_corr / (jnp.sqrt(second_new / second_corr) + epsilon)
+        n_b[z, h] = normed.astype(BF16)
         n_ring.start(h)
 
     def factors(k):
@@ -326,41 +365,49 @@
         rf_v[...] = rf_v[...] + (1.0 - shampoo_beta) * dot_nn(part, tile)
 
     def take_steps(k, h, fresh=False):
-        cols = slice(h * HALF, (h + 1) * HALF)
+        cols = slice(h * 256, (h + 1) * 256)
         term = dot_nt(qr_v[:, lanes(k)], n_b[k, h])
         sums[:, cols] = term if fresh else sums[:, cols] + term
 
-    rotate(0)
-    ql_ring.forward(2, 1)
+    for h in range(4):
+        rotate(h)
     rf_v[...] = shampoo_beta * rf_v[...]
-    take_steps(z, 0, True)
-    ql_ring.forward(3, 1)
-    rotate(1)
-    take_steps(z, 1, True)
+    for h in range(4):
+        take_steps(z, h, True)
     for s in range(3):
-        for h in range(2):
+        for h in range(4):
             n_ring.forward(s, h)
             take_steps(lax.rem(z + N - 1 - s, N), h)
             take_steps(lax.rem(z + 1 + s, N), h)
-            factors(lax.rem(z + 2 * s + h, N))
+            if h % 2 == 1:
+                factors(lax.rem(z + 2 * s + h // 2, N))
     factors(lax.rem(z + 6, N))
     factors(lax.rem(z + 7, N))
-    for h in range(2):
+    for h in range(4):
         n_ring.forward(3, h)
         take_steps(lax.rem(z + 4, N), h)
     back_v[...] = sums[...].astype(BF16)
 
     for d in range(2):
-        @pl.when(jnp.logical_not(jnp.logical_and(home, y_hi == d)))
+        @pl.when(direct(d))
         def _():
             acts_y(d).wait_send()
 
+    @pl.when(last)
+    def _():
+        acts_back().wait_send()
+
+    @pl.when(third)
+    def _():
+        acts_relay().wait_send()
+
     go_swap.wait_send()
-    for d in range(1, 4):
-        acts_x(d).wait_send()
+    for n in range(2):
+        for kind in range(3):
+            acts_x_out(n, kind).wait_send()
     for d in range(1, N):
         qr_out(d).wait_send()
-    for n in range(2):
+    for n in range(3):
         for a_ in (a, 1 - a):
             to_core(n, a_).wait_send()
         to_y(n).wait_send()
@@ -391,7 +438,7 @@
 def shards(acts, grad_out, left_factor, right_factor, left_basis, right_basis, moment, second):
     dma, vmem = pltpu.SemaphoreType.DMA, pltpu.VMEM
     hbm, on_chip = pl.BlockSpec(memory_space=pltpu.HBM), pl.BlockSpec(memory_space=pltpu.VMEM)
-    ring = [dma((2, 4, 2)), dma((2, 4, 2))]
+    halves, quarters = [dma((2, 4, 2))] * 2, [dma((2, 4, 4))] * 2
     arrays = (acts, grad_out, left_factor, right_factor, left_basis, right_basis, moment, second)
     shape = jax.ShapeDtypeStruct
     held = pl.pallas_call(
@@ -408,6 +455,7 @@
         out_specs=[on_chip] * 6,
         scratch_shapes=[
             vmem((T, W), BF16),
+            vmem((T, W), BF16),
             vmem((4, 2, T, W), BF16),
             vmem((2, 2, W, 2 * T), BF16),
             vmem((N, 2, T, W), BF16),
@@ -419,18 +467,18 @@
             vmem((W, B), BF16),
             vmem((N, W, W), BF16),
             vmem((W, B), BF16),
-            vmem((N, 2, W // 2, B), BF16),
+            vmem((N, 4, W // 4, B), BF16),
             vmem((W, B), BF16),
-            vmem((N, 2, HALF, W), BF16),
+            vmem((N, 4, 256, W), BF16),
             vmem((W, B), F32),
             dma((9,)),
-            dma((2,)), dma((2,)),
             dma((3,)), dma((3,)),
+            dma((2, 3)), dma((2, 3)),
             dma, dma,
             dma((N - 1,)), dma((N - 1,)),
-            dma((2, 2)), dma((2, 2)),
-            dma((2,)), dma((2,)),
-            *ring, *ring, *ring, *ring,
+            dma((3, 2)), dma((3, 2)),
+            dma((3,)), dma((3,)),
+            *halves, *halves, *quarters, *quarters,
         ],
         compiler_params=pltpu.CompilerParams(
             collective_id=0, has_side_effects=True, vmem_limit_bytes=40 * 1024 * 1024

time: 109 us -> 102 us (0.936)
  the two profiles are of different devices: /device:TPU:12 before, /device:TPU:16 now
where the time goes in v3:
time: 102 us
  Pallas kernels  101 us (99%)
    pallas_call x1, Pallas kernels, shards(): pl.pallas_call(kernel, out_shape=(shape((W, B), F32), shape((W, B), F32),...  99.6 us

profile of v3, /device:TPU:16, one launch (start us, length us, event | category | flops | bytes accessed | tf_op | source)
XLA Modules:
  0.0 101.9 jit_solution(6282455680183806185)
XLA Ops:
  0.6 99.6 %shard_map.119 = (f32[128,1024]{1,0:T(8,128)S(1)}, f32[128,1024]{1,0:T(8,128)S(1)}, f32[1024,128]{1,0:T(8,128)S(1)}, f32[1024,128]{1,0:T(8,128)S(1)}, bf16[128,1...) custom-call(bf16[256,128]{1,0:T(8,128)(2,1)} %acts_in.1, bf16[256,128]{1,0:T(8,128)(2,1)} %go_in.1, ...), custom_call_target="tpu_custom_call" | custom-call | tf_op jit(solution)/shard_map/pallas_call | solution.py:444
  100.2 1.7 %shard_map.120 = (f32[1,128,1024]{2,1,0:T(8,128)}, f32[1,128,1024]{2,1,0:T(8,128)}, f32[1024,128]{1,0:T(8,128)}, f32[1024,128]{1,0:T(8,128)}, bf16[1024,128]{1,0:T(8,128)(2,1)}) custom-call(f32[128,1024]{1,0:T(8,128)S(1)} %get-tuple-element.11.lf_v, f32[128,1024]{1,0:T(8,128)S(1)} %get-tuple-element.12.rf_v, f32[1024,128]{1,0:T(8,128)S(1)} %get-tuple-element.13.mo_v, ...), custom_call_target="tpu_custom_call" | custom-call | tf_op jit(solution)/shard_map/pallas_call | solution.py:487

commit v4 on v3

--- a/solution.py
+++ b/solution.py
@@ -336,8 +336,8 @@
     for s in range(3):
         for h in range(4):
             g_ring.forward(s, h)
-        if s < 2:
-            ql_ring.forward(2 + s, 1)
+        if s == 1:
+            ql_ring.forward(2, 1)
         mix(lax.rem(z + N - 1 - s, N))
         mix(lax.rem(z + 1 + s, N))
     for h in range(4):
@@ -370,6 +370,8 @@
         sums[:, cols] = term if fresh else sums[:, cols] + term
 
     for h in range(4):
+        if h == 2:
+            ql_ring.forward(3, 1)
         rotate(h)
     rf_v[...] = shampoo_beta * rf_v[...]
     for h in range(4):

time: 102 us -> 101 us (level)
    pallas_call x1, Pallas kernels: 99.6 us -> 98.4 us  [shards(): pl.pallas_call(kernel, out_shape=(shape((W, B), F32), shape((W, B), F32),...]
where the time goes in v4:
time: 101 us
  Pallas kernels  100 us (99%)
    pallas_call x1, Pallas kernels, shards(): pl.pallas_call(kernel, out_shape=(shape((W, B), F32), shape((W, B), F32),...  98.4 us

profile of v4, /device:TPU:16, one launch (start us, length us, event | category | flops | bytes accessed | tf_op | source)
XLA Modules:
  0.0 100.7 jit_solution(13878890637085309606)
XLA Ops:
  0.6 98.4 %shard_map.119 = (f32[128,1024]{1,0:T(8,128)S(1)}, f32[128,1024]{1,0:T(8,128)S(1)}, f32[1024,128]{1,0:T(8,128)S(1)}, f32[1024,128]{1,0:T(8,128)S(1)}, bf16[128,1...) custom-call(bf16[256,128]{1,0:T(8,128)(2,1)} %acts_in.1, bf16[256,128]{1,0:T(8,128)(2,1)} %go_in.1, ...), custom_call_target="tpu_custom_call" | custom-call | tf_op jit(solution)/shard_map/pallas_call | solution.py:446
  99.0 1.7 %shard_map.120 = (f32[1,128,1024]{2,1,0:T(8,128)}, f32[1,128,1024]{2,1,0:T(8,128)}, f32[1024,128]{1,0:T(8,128)}, f32[1024,128]{1,0:T(8,128)}, bf16[1024,128]{1,0:T(8,128)(2,1)}) custom-call(f32[128,1024]{1,0:T(8,128)S(1)} %get-tuple-element.11.lf_v, f32[128,1024]{1,0:T(8,128)S(1)} %get-tuple-element.12.rf_v, f32[1024,128]{1,0:T(8,128)S(1)} %get-tuple-element.13.mo_v, ...), custom_call_target="tpu_custom_call" | custom-call | tf_op jit(solution)/shard_map/pallas_call | solution.py:489
